TPU v7x, 32 devices: a whole 2x2x4 slice. The times are simulated.
32 devices in a mesh: row: 8 (over z, x), col: 4 (over y, core).
Axes of the slice: x: 2, y: 2, z: 4, core: 2. Of those that a mesh axis runs over, the one named last changes fastest.
Arguments:
- voltage: float32 [2, 4096, 16384], P(None, ('row', 'col')), may hold values from -6 to 6
- chirp_phase: float32 [16384, 4096], P(('row', 'col')), may hold values from -3.140625 to 3.140625
- filter_taps: float32 [8, 1024], replicated, may hold values from -0.0625 to 0.0625
Outputs:
- filterbank: float32 [2, 1024, 65536], P(None, None, ('row', 'col'))
All inputs are finite; a program needn't handle non-finite values.
Results may differ from a plain program's by a relative error of at most 0.00015.
Values sent between devices are 32-bit elements; how exact they have to be, the bound alone decides.
No kernel may reach another device: no remote copies, remote signals or barrier semaphores. Data moves between devices by JAX's collectives and lax.ppermute only.
A program may use at most 192 MiB of HBM per device.

v0:
```python
import math
import jax
import jax.numpy as jnp
from jax import lax
from jax.sharding import PartitionSpec as P

precise = lax.Precision.HIGHEST


def passed_along(block, axis, distance):
    devices = range(lax.axis_size(axis))
    route = [(i - distance, i) for i in devices if i - distance in devices]
    return lax.ppermute(block, axis, route)


def dft_table(radix, direction):
    digits = jnp.arange(radix, dtype=jnp.int32)
    product = digits[:, None] * digits[None, :] % radix
    turn = direction * 2.0 * math.pi / radix * product.astype(jnp.float32)
    cos_part = jnp.cos(turn)
    sin_part = jnp.sin(turn)
    upper = jnp.stack([cos_part, sin_part], axis=1)
    lower = jnp.stack([-sin_part, cos_part], axis=1)
    return jnp.stack([upper, lower], axis=0)


def complex_product(values, cos_part, sin_part):
    real_part = values[0] * cos_part - values[1] * sin_part
    imag_part = values[0] * sin_part + values[1] * cos_part
    return jnp.stack([real_part, imag_part])


def inner_twist(outer_radix, inner_radix, direction):
    outer_digits = jnp.arange(outer_radix, dtype=jnp.int32)
    inner_digits = jnp.arange(inner_radix, dtype=jnp.int32)
    length = outer_radix * inner_radix
    product = outer_digits[:, None] * inner_digits[None, :] % length
    turn = direction * 2.0 * math.pi / length * product.astype(jnp.float32)
    return (jnp.cos(turn), jnp.sin(turn))


def dft_rows(values, direction):
    length = values.shape[1]
    column_count = values.shape[2]
    inner_radix = min(length, 128)
    outer_radix = length // inner_radix
    blocked = values.reshape(2, outer_radix, inner_radix, column_count)
    partial_value = jnp.einsum(
        "cadk,cabm->dkbm", dft_table(outer_radix, direction), blocked, precision=precise
    )
    cos_part, sin_part = inner_twist(outer_radix, inner_radix, direction)
    partial_value = complex_product(partial_value, cos_part[:, :, None], sin_part[:, :, None])
    result = jnp.einsum(
        "cbdq,ckbm->dqkm", dft_table(inner_radix, direction), partial_value, precision=precise
    )
    return result.reshape(2, length, column_count)


def dft_cols(values, direction):
    length = values.shape[2]
    row_count = values.shape[1]
    inner_radix = min(length, 128)
    outer_radix = length // inner_radix
    blocked = values.reshape(2, row_count, outer_radix, inner_radix)
    partial_value = jnp.einsum(
        "cadk,cmab->dmkb", dft_table(outer_radix, direction), blocked, precision=precise
    )
    cos_part, sin_part = inner_twist(outer_radix, inner_radix, direction)
    partial_value = complex_product(partial_value, cos_part, sin_part)
    result = jnp.einsum(
        "cbdq,cmkb->dmqk", dft_table(inner_radix, direction), partial_value, precision=precise
    )
    return result.reshape(2, row_count, length)


def rotate(values, row_index, col_index, total, direction, factor):
    product = row_index[:, None] * col_index[None, :] % total
    turn = direction * 2.0 * math.pi / total * product.astype(jnp.float32)
    return complex_product(values, factor * jnp.cos(turn), factor * jnp.sin(turn))


def spread(values):
    return lax.all_to_all(values, ("row", "col"), split_axis=2, concat_axis=1, tiled=True)


def collect(values):
    return lax.all_to_all(values, ("row", "col"), split_axis=1, concat_axis=2, tiled=True)


def local(voltage, chirp_phase, filter_taps):
    device_count = lax.axis_size("row") * lax.axis_size("col")
    device = lax.axis_index(("row", "col"))
    local_rows = voltage.shape[1]
    total_rows = local_rows * device_count
    total_cols = voltage.shape[2]
    local_cols = total_cols // device_count
    total = total_rows * total_cols
    signal = spread(voltage)
    signal = dft_rows(signal, -1.0)
    row_index = jnp.arange(total_rows, dtype=jnp.int32)
    col_index = device * local_cols + jnp.arange(local_cols, dtype=jnp.int32)
    signal = rotate(signal, row_index, col_index, total, -1.0, 1.0)
    signal = collect(signal)
    signal = dft_cols(signal, -1.0)
    turned_phase = jnp.transpose(chirp_phase)
    local_phase = lax.all_to_all(
        turned_phase, ("row", "col"), split_axis=0, concat_axis=1, tiled=True
    )
    signal = complex_product(signal, jnp.cos(local_phase), jnp.sin(local_phase))
    signal = dft_cols(signal, 1.0)
    row_index = device * local_rows + jnp.arange(local_rows, dtype=jnp.int32)
    col_index = jnp.arange(total_cols, dtype=jnp.int32)
    signal = rotate(signal, row_index, col_index, total, 1.0, 1.0 / total)
    signal = spread(signal)
    signal = dft_rows(signal, 1.0)
    signal = collect(signal)
    tap_count = filter_taps.shape[0]
    channel_count = filter_taps.shape[1]
    samples = signal.reshape(2, local_rows * total_cols)
    frame_count = samples.shape[1] // channel_count
    frames = samples.reshape(2, frame_count, channel_count)
    history = passed_along(frames[:, frame_count - tap_count + 1 :, :], ("row", "col"), 1)
    extended = jnp.concatenate([history, frames], axis=1)
    turned = jnp.transpose(extended, (0, 2, 1))
    weighted = jnp.zeros((2, channel_count, frame_count), jnp.float32)
    for tap_delay in range(tap_count):
        offset = tap_count - 1 - tap_delay
        weighted = (
            weighted
            + filter_taps[tap_delay][None, :, None] * turned[:, :, offset : offset + frame_count]
        )
    return dft_rows(weighted, -1.0)


def solution(mesh):
    in_specs = (P(None, ("row", "col"), None), P(("row", "col"), None), P())
    out_specs = P(None, None, ("row", "col"))
    return jax.shard_map(local, mesh=mesh, in_specs=in_specs, out_specs=out_specs, check_vma=False)
```

profile of v0, /device:TPU:6, one launch (start us, length us, event | category | flops | bytes accessed | tf_op | source)
XLA Modules:
  0.0 2393.4 jit_solution(8709069159866349502)
XLA Ops:
  0.0 24.9 %copy.169 = f32[2,128,16384]{1,0,2:T(2,128)} copy(f32[2,128,16384]{2,1,0:T(8,128)} %param.3) | data formatting | bytes 33554432 | tf_op args[0]
  40.1 370.0 %all-to-all-done = f32[2,128,16384]{1,0,2:T(2,128)} async-done(((f32[2,128,16384]{1,0,2:T(2,128)}), f32[2,128,16384]{1,0,2:T(2,128)}, u32[]{:S(2)}, u32[]{:S(2)}) %all-to-all-start) | async-done | bytes 16777248 | tf_op jit(solution)/shard_map/all_to_all | solution.py:83
  414.6 20.2 copy.234
  434.8 21.7 fusion.71
  466.8 28.9 %fusion.59 = f32[2,128,32,512]{3,1,2,0:T(8,128)S(1)} fusion(f32[2,32,128,512]{3,1,2,0:T(8,128)S(1)} %pad_maximum_fusion, f32[1,128,2,128]{1,3,0,2:T(8,128)S(1)} %get-tuple-element.30, f32[1,128,2,128]{1,3,0,2:T(8,128)S(1)} %get-tuple-element.29), kind=kOutput, calls=%fused_computation.103 | convolution fusion | flops 12884967424 | bytes 33816576 | tf_op jit(solution)/shard_map/cbdq,ckbm->dqkm/dot_general | solution.py:53
  519.2 36.9 %fusion.51 = (f32[1,4096,512]{2,1,0:T(8,128)S(1)}, f32[1,4096,512]{2,1,0:T(8,128)S(1)}) fusion(f32[1,128,32,512]{3,2,1,0:T(8,128)S(1)} %copy.173, f32[1,128,32,512]{3,2,1,0:T(8,128)S(1)} %copy.172, s32[512]{0:T(512)S(1)} %iota_add_fusion), kind=kLoop, calls=%fused_computation.77 | loop fusion | flops 41943040 | bytes 33556480 | tf_op jit(solution)/shard_map/sub | solution.py:28
  557.9 32.2 %copy.174 = f32[2,4096,512]{2,0,1:T(2,128)} copy(f32[2,4096,512]{2,1,0:T(8,128)S(1)} %pad_maximum_fusion.1) | data formatting | bytes 33554432 | tf_op jit(solution)/shard_map/stack | solution.py:30
  607.9 31.5 %sine_bitcast_fusion = (f32[128,32,512]{2,0,1:T(8,128)}, f32[128,32,512]{2,0,1:T(8,128)}) fusion(f32[32,128,512]{2,1,0:T(8,128)} %all-to-all-done.2), kind=kLoop, calls=%fused_computation.93 | loop fusion | bytes 25165824 | tf_op jit(solution)/shard_map/sin | solution.py:109
  676.1 309.5 %all-to-all-done.1 = f32[2,4096,512]{2,0,1:T(2,128)} async-done(((f32[2,4096,512]{2,0,1:T(2,128)}), f32[2,4096,512]{2,0,1:T(2,128)}, u32[]{:S(2)}, u32[]{:S(2)}) %all-to-all-start.1) | async-done | bytes 16777248 | tf_op jit(solution)/shard_map/all_to_all | solution.py:87
  1059.4 31.5 %fusion.36 = f32[2,128,128,128]{2,3,0,1:T(8,128)} fusion(f32[1,128,128,128]{2,3,0,1:T(8,128)} %get-tuple-element.14, f32[1,128,128,128]{2,3,0,1:T(8,128)} %get-tuple-element.13, f32[1,128,2,128]{1,3,0,2:T(8,128)S(1)} %get-tuple-element.30, f32[1,128,2,128]{1,3,0,2:T(8,128)S(1)} %get-tuple-element.29), kind=kOutput, calls=%fused_computation.59 | convolution fusion | flops 12889161728 | bytes 33816576 | tf_op jit(solution)/shard_map/cbdq,cmkb->dmqk/dot_general | solution.py:70
  1134.3 31.7 %fusion.40 = f32[2,128,128,128]{2,3,0,1:T(8,128)S(1)} fusion(f32[1,128,128,128]{2,3,0,1:T(8,128)} %get-tuple-element.12, f32[1,128,128,128]{2,3,0,1:T(8,128)} %get-tuple-element.11, f32[1,128,2,128]{1,3,2,0:T(8,128)S(1)} %get-tuple-element.28, f32[1,128,2,128]{1,3,2,0:T(8,128)S(1)} %get-tuple-element.27), kind=kOutput, calls=%fused_computation.61 | convolution fusion | flops 12889161728 | bytes 33816576 | tf_op jit(solution)/shard_map/cbdq,cmkb->dmqk/dot_general | solution.py:70
  1191.5 36.6 %fusion.49 = (f32[1,128,16384]{1,2,0:T(8,128)S(1)}, f32[1,128,16384]{1,2,0:T(8,128)S(1)}) fusion(f32[1,128,128,128]{1,3,2,0:T(8,128)} %copy.192, f32[1,128,128,128]{1,3,2,0:T(8,128)} %copy.191, s32[128]{0:T(128)S(1)} %iota_add_fusion.1), kind=kLoop, calls=%fused_computation.71 | loop fusion | flops 46137344 | bytes 33554944 | tf_op jit(solution)/shard_map/sub | solution.py:28
  1229.2 61.7 %copy.193 = f32[2,128,16384]{1,0,2:T(2,128)} copy(f32[2,128,16384]{1,2,0:T(8,128)S(1)} %pad_maximum_fusion.2) | data formatting | bytes 33554432 | tf_op jit(solution)/shard_map/stack | solution.py:30
  1295.5 377.9 %all-to-all-done.3 = f32[2,128,16384]{1,0,2:T(2,128)} async-done(((f32[2,128,16384]{1,0,2:T(2,128)}), f32[2,128,16384]{1,0,2:T(2,128)}, u32[]{:S(2)}, u32[]{:S(2)}) %all-to-all-start.3) | async-done | bytes 16777248 | tf_op jit(solution)/shard_map/all_to_all | solution.py:83
  1673.4 20.1 copy.247
  1693.4 21.7 fusion.74
  1725.4 28.9 %fusion.62 = f32[2,128,32,512]{3,1,2,0:T(8,128)S(1)} fusion(f32[2,32,128,512]{3,1,2,0:T(8,128)S(1)} %pad_maximum_fusion.3, f32[1,128,2,128]{1,3,2,0:T(8,128)S(1)} %get-tuple-element.28, f32[1,128,2,128]{1,3,2,0:T(8,128)S(1)} %get-tuple-element.27), kind=kOutput, calls=%fused_computation.104 | convolution fusion | flops 12884967424 | bytes 33816576 | tf_op jit(solution)/shard_map/cbdq,ckbm->dqkm/dot_general | solution.py:53
  1754.3 20.1 copy.198
  1774.4 28.6 %copy.199 = f32[2,4096,512]{2,0,1:T(2,128)} copy(f32[2,4096,512]{2,1,0:T(8,128)} %bitcast.229) | data formatting | bytes 33554432 | tf_op jit(solution)/shard_map/reshape | solution.py:56
  1807.3 377.8 %all-to-all-done.4 = f32[2,4096,512]{2,0,1:T(2,128)} async-done(((f32[2,4096,512]{2,0,1:T(2,128)}), f32[2,4096,512]{2,0,1:T(2,128)}, u32[]{:S(2)}, u32[]{:S(2)}) %all-to-all-start.4) | async-done | bytes 16777248 | tf_op jit(solution)/shard_map/all_to_all | solution.py:87
  2240.3 50.0 %fusion = f32[2,1024,2048]{1,2,0:T(8,128)} fusion(f32[2,1024,2055]{1,2,0:T(8,128)} %maximum_bitcast_fusion, f32[1024]{0:T(1024)S(1)} %bitcast.241, f32[1024]{0:T(1024)S(1)} %bitcast.242, f32[1024]{0:T(1024)S(1)} %bitcast.236, f32[1024]{0:T(1024)S(1)} %bitcast.237, f32[1024]{0:T(1024)S(1)} %bitcast.238, f32[1024]{0:T(1024)S(1)} %bitcast.239, ...), kind=kLoop, calls=%fused_computation.2 | loop fusion | flops 62914560 | bytes 151027712 | tf_op jit(solution)/shard_map/add | solution.py:129
  2307.7 32.0 %fusion.65 = f32[2,8,128,2048]{3,1,2,0:T(8,128)} fusion(f32[2,8,128,2048]{3,2,1,0:T(8,128)} %bitcast.231, f32[1,8,2,8]{1,3,0,2:T(8,128)S(1)} %copy.167, f32[1,8,2,8]{1,3,0,2:T(8,128)S(1)} %copy.166), kind=kOutput, calls=%fused_computation.105 | convolution fusion | flops 805306624 | bytes 33555456 | tf_op jit(solution)/shard_map/cadk,cabm->dkbm/dot_general | solution.py:48
  2349.0 23.7 fusion.68
  2372.7 20.2 copy.278
  (78 shorter events, 354.2 us)
Async XLA Ops:
  24.9 385.2 %all-to-all-start = ((f32[2,128,16384]{1,0,2:T(2,128)}), f32[2,128,16384]{1,0,2:T(2,128)}, u32[]{:S(2)}, u32[]{:S(2)}) async-start(f32[2,128,16384]{1,0,2:T(2,128)} %copy.169), calls=%async_computation | async-start | bytes 33554432 | tf_op jit(solution)/shard_map/all_to_all | solution.py:83
  410.1 191.6 %all-to-all-start.2 = ((f32[32,128,512]{2,1,0:T(8,128)}), f32[32,128,512]{2,1,0:T(8,128)}, u32[]{:S(2)}, u32[]{:S(2)}) async-start(f32[32,128,512]{2,1,0:T(8,128)} %bitcast.232), calls=%async_computation.2 | async-start | bytes 16777216 | tf_op jit(solution)/shard_map/all_to_all | solution.py:106
  414.6 644.8 %copy-start = (f32[1,128,2,128]{1,3,0,2:T(8,128)}, f32[1,128,2,128]{1,3,0,2:T(8,128)S(1)}, u32[]{:S(2)}) copy-start(f32[1,128,2,128]{1,3,0,2:T(8,128)S(1)} %get-tuple-element.29) | copy-start | bytes 393220
  414.6 644.8 %copy-start.2 = (f32[1,128,2,128]{1,3,0,2:T(8,128)}, f32[1,128,2,128]{1,3,0,2:T(8,128)S(1)}, u32[]{:S(2)}) copy-start(f32[1,128,2,128]{1,3,0,2:T(8,128)S(1)} %get-tuple-element.30) | copy-start | bytes 393220
  601.7 383.8 %all-to-all-start.1 = ((f32[2,4096,512]{2,0,1:T(2,128)}), f32[2,4096,512]{2,0,1:T(2,128)}, u32[]{:S(2)}, u32[]{:S(2)}) async-start(f32[2,4096,512]{2,0,1:T(2,128)} %copy.174), calls=%async_computation.1 | async-start | bytes 33554432 | tf_op jit(solution)/shard_map/all_to_all | solution.py:87
  1291.0 382.4 %all-to-all-start.3 = ((f32[2,128,16384]{1,0,2:T(2,128)}), f32[2,128,16384]{1,0,2:T(2,128)}, u32[]{:S(2)}, u32[]{:S(2)}) async-start(f32[2,128,16384]{1,0,2:T(2,128)} %copy.193), calls=%async_computation.3 | async-start | bytes 33554432 | tf_op jit(solution)/shard_map/all_to_all | solution.py:83
  1803.0 4.2 copy-start.4
  1803.0 382.1 %all-to-all-start.4 = ((f32[2,4096,512]{2,0,1:T(2,128)}), f32[2,4096,512]{2,0,1:T(2,128)}, u32[]{:S(2)}, u32[]{:S(2)}) async-start(f32[2,4096,512]{2,0,1:T(2,128)} %copy.199), calls=%async_computation.4 | async-start | bytes 33554432 | tf_op jit(solution)/shard_map/all_to_all | solution.py:87
  2222.9 5.6 collective-permute-start
  2346.9 2.0 copy-start.1
  2346.9 2.0 copy-start.3
where the time goes:
time: 2410 us; the launch traced here: 2390 us
  waiting for transfers between devices  1450 us (60%)
  local copies, waits for them, and re-layouts  460 us (19%)
  matrix products  255 us (11%)
  other arithmetic  204 us (8%)
  starting transfers between devices  24.3 us (1%)
    all_to_all x2, waiting for transfers between devices, spread(): lax.all_to_all(values, ('row', 'col'), split_axis=2, concat_axis=1, tiled...  748 us
    all_to_all x2, waiting for transfers between devices, collect(): lax.all_to_all(values, ('row', 'col'), split_axis=1, concat_axis=2, tiled...  687 us
    sub x8, other arithmetic, complex_product(): real_part = values[0] * cos_part - values[1] * sin_part  128 us
    another operation x2, local copies, waits for them, and re-layouts, complex_product(): return jnp.stack([real_part, imag_part])  94 us
    dot_general x3, matrix products, dft_rows(): jnp.einsum('cbdq,ckbm->dqkm', dft_table(inner_radix, direction), partial_...  81.5 us
    dot_general x3, matrix products, dft_rows(): jnp.einsum('cadk,cabm->dkbm', dft_table(outer_radix, direction), blocked,...  75.5 us
    dot_general x2, matrix products, dft_cols(): jnp.einsum('cbdq,cmkb->dmqk', dft_table(inner_radix, direction), partial_...  63.2 us
    add x1, other arithmetic, local(): weighted + filter_taps[tap_delay][None, :, None] * turned[:, :, offset:of...  50 us
  transfers between devices with their start and end apart: 6, of which 6 were waited for; matrix products, arithmetic and copies ran while one was open for 11% of the time, Pallas kernels for 0%

commit v1 on v0

--- a/solution.py
+++ b/solution.py
@@ -80,7 +80,15 @@
 
 
 def spread(values):
-    return lax.all_to_all(values, ("row", "col"), split_axis=2, concat_axis=1, tiled=True)
+    return jnp.concatenate(
+        lax.all_to_all(
+            jnp.stack(jnp.split(values, lax.axis_size(("row", "col")), axis=2)),
+            ("row", "col"),
+            0,
+            0,
+        ),
+        axis=1,
+    )
 
 
 def collect(values):

time: 2410 us -> 2420 us (level)
  local copies, waits for them, and re-layouts: 460 us -> 422 us
  other arithmetic: 204 us -> 229 us
    another operation x2 -> x1, local copies, waits for them, and re-layouts: 94 us -> 32.2 us  [complex_product(): return jnp.stack([real_part, imag_part])]
    all_to_all x2 -> x0, local copies, waits for them, and re-layouts: 40.2 us -> none  [spread(): lax.all_to_all(values, ('row', 'col'), split_axis=2, concat_axis=1, tiled...]
    unnamed x12 -> x50, local copies, waits for them, and re-layouts: 34 us -> 62.3 us
    another operation x0 -> x2, local copies, waits for them, and re-layouts: none -> 26.2 us  [spread(): jnp.stack(jnp.split(values, lax.axis_size(('row', 'col')), axis=2))]
    unnamed x0 -> x31, other arithmetic: none -> 25.6 us
  transfers between devices with their start and end apart: 6 -> 6, of which waited for: 6 -> 6; matrix products, arithmetic and copies ran while one was open for 11% -> 10% of each run, Pallas kernels for 0% -> 0%
where the time goes in v1:
time: 2420 us; the launch traced here: 2410 us
  waiting for transfers between devices  1460 us (60%)
  local copies, waits for them, and re-layouts  422 us (17%)
  matrix products  277 us (11%)
  other arithmetic  229 us (9%)
    all_to_all x2, waiting for transfers between devices, spread(): lax.all_to_all(jnp.stack(jnp.split(values, lax.axis_size(('row', 'col')),...  748 us
    all_to_all x2, waiting for transfers between devices, collect(): lax.all_to_all(values, ('row', 'col'), split_axis=1, concat_axis=2, tiled...  687 us
    sub x8, other arithmetic, complex_product(): real_part = values[0] * cos_part - values[1] * sin_part  128 us
    dot_general x3, matrix products, dft_rows(): jnp.einsum('cadk,cabm->dkbm', dft_table(outer_radix, direction), blocked,...  97.8 us
    dot_general x3, matrix products, dft_rows(): jnp.einsum('cbdq,ckbm->dqkm', dft_table(inner_radix, direction), partial_...  81.5 us
    dot_general x2, matrix products, dft_cols(): jnp.einsum('cbdq,cmkb->dmqk', dft_table(inner_radix, direction), partial_...  63 us
    unnamed x50, local copies, waits for them, and re-layouts  62.3 us
    add x1, other arithmetic, local(): weighted + filter_taps[tap_delay][None, :, None] * turned[:, :, offset:of...  50 us
  transfers between devices with their start and end apart: 6, of which 6 were waited for; matrix products, arithmetic and copies ran while one was open for 10% of the time, Pallas kernels for 0%

profile of v1, /device:TPU:6, one launch (start us, length us, event | category | flops | bytes accessed | tf_op | source)
XLA Modules:
  0.0 2412.0 jit_solution(8033772466038895484)
XLA Ops:
  79.5 370.0 %all-to-all-done = f32[32,2,128,512]{3,1,2,0:T(2,128)} async-done(((f32[32,2,128,512]{3,1,2,0:T(2,128)}), f32[32,2,128,512]{3,1,2,0:T(2,128)}, u32[]{:S(2)}, u32[]{:S(2)}) %all-to-all-start) | async-done | bytes 16777248 | tf_op jit(solution)/shard_map/all_to_all | solution.py:84
  454.0 32.8 %fusion.73 = f32[2,32,128,512]{3,1,2,0:T(8,128)} fusion(f32[32,2,128,512]{3,1,2,0:T(2,128)} %all-to-all-done, f32[1,32,2,32]{1,3,0,2:T(8,128)S(1)} %get-tuple-element.74, f32[1,32,2,32]{1,3,0,2:T(8,128)S(1)} %get-tuple-element.73), kind=kOutput, calls=%fused_computation.170 | convolution fusion | flops 3221229568 | bytes 33570816 | tf_op jit(solution)/shard_map/cadk,cabm->dkbm/dot_general | solution.py:48
  497.1 28.9 %fusion.61 = f32[2,128,32,512]{3,1,2,0:T(8,128)S(1)} fusion(f32[2,32,128,512]{3,1,2,0:T(8,128)S(1)} %pad_maximum_fusion, f32[1,128,2,128]{1,3,0,2:T(8,128)S(1)} %get-tuple-element.62, f32[1,128,2,128]{1,3,0,2:T(8,128)S(1)} %get-tuple-element.61), kind=kOutput, calls=%fused_computation.166 | convolution fusion | flops 12884967424 | bytes 33816576 | tf_op jit(solution)/shard_map/cbdq,ckbm->dqkm/dot_general | solution.py:53
  549.5 36.9 %fusion.53 = (f32[1,4096,512]{2,1,0:T(8,128)S(1)}, f32[1,4096,512]{2,1,0:T(8,128)S(1)}) fusion(f32[1,128,32,512]{3,2,1,0:T(8,128)S(1)} %copy.458, f32[1,128,32,512]{3,2,1,0:T(8,128)S(1)} %copy.457, s32[512]{0:T(512)S(1)} %iota_add_fusion), kind=kLoop, calls=%fused_computation.140 | loop fusion | flops 41943040 | bytes 33556480 | tf_op jit(solution)/shard_map/sub | solution.py:28
  588.3 32.2 %copy.459 = f32[2,4096,512]{2,0,1:T(2,128)} copy(f32[2,4096,512]{2,1,0:T(8,128)S(1)} %pad_maximum_fusion.1) | data formatting | bytes 33554432 | tf_op jit(solution)/shard_map/stack | solution.py:30
  620.5 20.7 all-to-all-done.2
  647.5 31.6 %sine_bitcast_fusion = (f32[128,32,512]{2,0,1:T(8,128)}, f32[128,32,512]{2,0,1:T(8,128)}) fusion(f32[32,128,512]{2,1,0:T(8,128)} %all-to-all-done.2), kind=kLoop, calls=%fused_computation.156 | loop fusion | bytes 25165824 | tf_op jit(solution)/shard_map/sin | solution.py:117
  715.8 309.3 %all-to-all-done.1 = f32[2,4096,512]{2,0,1:T(2,128)} async-done(((f32[2,4096,512]{2,0,1:T(2,128)}), f32[2,4096,512]{2,0,1:T(2,128)}, u32[]{:S(2)}, u32[]{:S(2)}) %all-to-all-start.1) | async-done | bytes 16777248 | tf_op jit(solution)/shard_map/all_to_all | solution.py:95
  1099.0 31.3 %fusion.38 = f32[2,128,128,128]{2,3,0,1:T(8,128)} fusion(f32[1,128,128,128]{2,3,0,1:T(8,128)} %get-tuple-element.14, f32[1,128,128,128]{2,3,0,1:T(8,128)} %get-tuple-element.13, f32[1,128,2,128]{1,3,0,2:T(8,128)S(1)} %get-tuple-element.62, f32[1,128,2,128]{1,3,0,2:T(8,128)S(1)} %get-tuple-element.61), kind=kOutput, calls=%fused_computation.122 | convolution fusion | flops 12889161728 | bytes 33816576 | tf_op jit(solution)/shard_map/cbdq,cmkb->dmqk/dot_general | solution.py:70
  1130.3 18.9 multiply_subtract_fusion.3
  1173.9 31.7 %fusion.42 = f32[2,128,128,128]{2,3,0,1:T(8,128)S(1)} fusion(f32[1,128,128,128]{2,3,0,1:T(8,128)} %get-tuple-element.12, f32[1,128,128,128]{2,3,0,1:T(8,128)} %get-tuple-element.11, f32[1,128,2,128]{1,3,2,0:T(8,128)S(1)} %get-tuple-element.60, f32[1,128,2,128]{1,3,2,0:T(8,128)S(1)} %get-tuple-element.59), kind=kOutput, calls=%fused_computation.124 | convolution fusion | flops 12889161728 | bytes 33816576 | tf_op jit(solution)/shard_map/cbdq,cmkb->dmqk/dot_general | solution.py:70
  1231.0 36.6 %fusion.51 = (f32[1,128,16384]{1,2,0:T(8,128)S(1)}, f32[1,128,16384]{1,2,0:T(8,128)S(1)}) fusion(f32[1,128,128,128]{1,3,2,0:T(8,128)} %copy.477, f32[1,128,128,128]{1,3,2,0:T(8,128)} %copy.476, s32[128]{0:T(128)S(1)} %iota_add_fusion.1), kind=kLoop, calls=%fused_computation.134 | loop fusion | flops 46137344 | bytes 33554944 | tf_op jit(solution)/shard_map/sub | solution.py:28
  1294.1 25.0 %copy.478 = f32[32,2,128,512]{3,1,2,0:T(2,128)} copy(f32[32,2,128,512]{2,3,1,0:T(8,128)} %fusion.113) | data formatting | bytes 33554432 | tf_op jit(solution)/shard_map/stack | solution.py:85
  1323.1 378.0 %all-to-all-done.3 = f32[32,2,128,512]{3,1,2,0:T(2,128)} async-done(((f32[32,2,128,512]{3,1,2,0:T(2,128)}), f32[32,2,128,512]{3,1,2,0:T(2,128)}, u32[]{:S(2)}, u32[]{:S(2)}) %all-to-all-start.3) | async-done | bytes 16777248 | tf_op jit(solution)/shard_map/all_to_all | solution.py:84
  1701.2 32.7 %fusion.76 = f32[2,32,128,512]{3,1,2,0:T(8,128)} fusion(f32[32,2,128,512]{3,1,2,0:T(2,128)} %all-to-all-done.3, f32[1,32,2,32]{1,3,2,0:T(8,128)S(1)} %get-tuple-element.72, f32[1,32,2,32]{1,3,2,0:T(8,128)S(1)} %get-tuple-element.71), kind=kOutput, calls=%fused_computation.171 | convolution fusion | flops 3221229568 | bytes 33570816 | tf_op jit(solution)/shard_map/cadk,cabm->dkbm/dot_general | solution.py:48
  1744.2 28.9 %fusion.64 = f32[2,128,32,512]{3,1,2,0:T(8,128)S(1)} fusion(f32[2,32,128,512]{3,1,2,0:T(8,128)S(1)} %pad_maximum_fusion.2, f32[1,128,2,128]{1,3,2,0:T(8,128)S(1)} %copy-done.7, f32[1,128,2,128]{1,3,2,0:T(8,128)S(1)} %copy-done.5), kind=kOutput, calls=%fused_computation.167 | convolution fusion | flops 12884967424 | bytes 33816576 | tf_op jit(solution)/shard_map/cbdq,ckbm->dqkm/dot_general | solution.py:53
  1773.1 20.1 copy.483
  1793.2 28.6 %copy.484 = f32[2,4096,512]{2,0,1:T(2,128)} copy(f32[2,4096,512]{2,1,0:T(8,128)} %bitcast.421) | data formatting | bytes 33554432 | tf_op jit(solution)/shard_map/reshape | solution.py:56
  1826.0 377.8 %all-to-all-done.4 = f32[2,4096,512]{2,0,1:T(2,128)} async-done(((f32[2,4096,512]{2,0,1:T(2,128)}), f32[2,4096,512]{2,0,1:T(2,128)}, u32[]{:S(2)}, u32[]{:S(2)}) %all-to-all-start.4) | async-done | bytes 16777248 | tf_op jit(solution)/shard_map/all_to_all | solution.py:95
  2221.6 19.2 reshape_reshape.3
  2259.1 50.0 %fusion = f32[2,1024,2048]{1,2,0:T(8,128)} fusion(f32[2,1024,2055]{1,2,0:T(8,128)} %maximum_bitcast_fusion, f32[1024]{0:T(1024)S(1)} %bitcast.433, f32[1024]{0:T(1024)S(1)} %bitcast.434, f32[1024]{0:T(1024)S(1)} %bitcast.428, f32[1024]{0:T(1024)S(1)} %bitcast.429, f32[1024]{0:T(1024)S(1)} %bitcast.430, f32[1024]{0:T(1024)S(1)} %bitcast.431, ...), kind=kLoop, calls=%fused_computation.64 | loop fusion | flops 62914560 | bytes 151027712 | tf_op jit(solution)/shard_map/add | solution.py:137
  2326.4 32.2 %fusion.67 = f32[2,8,128,2048]{3,1,2,0:T(8,128)} fusion(f32[2,8,128,2048]{3,2,1,0:T(8,128)} %bitcast.423, f32[1,8,2,8]{1,3,0,2:T(8,128)S(1)} %copy.421, f32[1,8,2,8]{1,3,0,2:T(8,128)S(1)} %copy.420), kind=kOutput, calls=%fused_computation.168 | convolution fusion | flops 805306624 | bytes 33555456 | tf_op jit(solution)/shard_map/cadk,cabm->dkbm/dot_general | solution.py:48
  2367.9 23.7 fusion.70
  2391.6 20.2 copy.701
  (148 shorter events, 394.0 us)
Async XLA Ops:
  64.3 385.2 %all-to-all-start = ((f32[32,2,128,512]{3,1,2,0:T(2,128)}), f32[32,2,128,512]{3,1,2,0:T(2,128)}, u32[]{:S(2)}, u32[]{:S(2)}) async-start(f32[32,2,128,512]{3,1,2,0:T(2,128)} %fusion.114), calls=%async_computation | async-start | bytes 33554432 | tf_op jit(solution)/shard_map/all_to_all | solution.py:84
  449.5 191.7 %all-to-all-start.2 = ((f32[32,128,512]{2,1,0:T(8,128)}), f32[32,128,512]{2,1,0:T(8,128)}, u32[]{:S(2)}, u32[]{:S(2)}) async-start(f32[32,128,512]{2,1,0:T(8,128)} %bitcast.424), calls=%async_computation.2 | async-start | bytes 16777216 | tf_op jit(solution)/shard_map/all_to_all | solution.py:114
  454.0 645.0 %copy-start = (f32[1,128,2,128]{1,3,0,2:T(8,128)}, f32[1,128,2,128]{1,3,0,2:T(8,128)S(1)}, u32[]{:S(2)}) copy-start(f32[1,128,2,128]{1,3,0,2:T(8,128)S(1)} %get-tuple-element.61) | copy-start | bytes 393220
  454.0 645.0 %copy-start.2 = (f32[1,128,2,128]{1,3,0,2:T(8,128)}, f32[1,128,2,128]{1,3,0,2:T(8,128)S(1)}, u32[]{:S(2)}) copy-start(f32[1,128,2,128]{1,3,0,2:T(8,128)S(1)} %get-tuple-element.62) | copy-start | bytes 393220
  641.2 384.0 %all-to-all-start.1 = ((f32[2,4096,512]{2,0,1:T(2,128)}), f32[2,4096,512]{2,0,1:T(2,128)}, u32[]{:S(2)}, u32[]{:S(2)}) async-start(f32[2,4096,512]{2,0,1:T(2,128)} %copy.459), calls=%async_computation.1 | async-start | bytes 33554432 | tf_op jit(solution)/shard_map/all_to_all | solution.py:95
  647.5 526.4 %copy-start.4 = (f32[1,128,2,128]{1,3,2,0:T(8,128)}, f32[1,128,2,128]{1,3,2,0:T(8,128)S(1)}, u32[]{:S(2)}) copy-start(f32[1,128,2,128]{1,3,2,0:T(8,128)S(1)} %get-tuple-element.59) | copy-start | bytes 393220
  647.5 526.4 %copy-start.6 = (f32[1,128,2,128]{1,3,2,0:T(8,128)}, f32[1,128,2,128]{1,3,2,0:T(8,128)S(1)}, u32[]{:S(2)}) copy-start(f32[1,128,2,128]{1,3,2,0:T(8,128)S(1)} %get-tuple-element.60) | copy-start | bytes 393220
  1319.0 382.1 %all-to-all-start.3 = ((f32[32,2,128,512]{3,1,2,0:T(2,128)}), f32[32,2,128,512]{3,1,2,0:T(2,128)}, u32[]{:S(2)}, u32[]{:S(2)}) async-start(f32[32,2,128,512]{3,1,2,0:T(2,128)} %copy.478), calls=%async_computation.3 | async-start | bytes 33554432 | tf_op jit(solution)/shard_map/all_to_all | solution.py:84
  1740.9 3.3 copy-start.5
  1740.9 3.3 copy-start.7
  1821.8 4.2 copy-start.8
  1821.8 382.1 %all-to-all-start.4 = ((f32[2,4096,512]{2,0,1:T(2,128)}), f32[2,4096,512]{2,0,1:T(2,128)}, u32[]{:S(2)}, u32[]{:S(2)}) async-start(f32[2,4096,512]{2,0,1:T(2,128)} %copy.484), calls=%async_computation.4 | async-start | bytes 33554432 | tf_op jit(solution)/shard_map/all_to_all | solution.py:95
  2241.7 5.6 collective-permute-start
  2365.9 2.0 copy-start.1
  2365.9 2.0 copy-start.3
